TPU v7x, 512 devices: a whole 4x4x16 slice. The times are simulated.
512 devices in a mesh: grp: 16 (over z), dp: 32 (over x, y, core).
Axes of the slice: x: 4, y: 4, z: 16, core: 2. Of those that a mesh axis runs over, the one named last changes fastest.
Arguments:
- tokens: bfloat16 [65536, 3584], P(('grp', 'dp')), may hold values from -120 to 120, as said below
- lengths: int32 [512, 4], P(('grp', 'dp')), may hold values from 0 to 128, as said below
- dest: int32 [512, 4], P(('grp', 'dp')), may hold values from -1 to 15, as said below
- gain: float32 [3584], replicated, may hold values from 0.5 to 1.5
- weight: bfloat16 [3584, 10240], P('dp', 'grp'), may hold values from -0.09375 to 0.09375
Outputs:
- projected: bfloat16 [32768, 10240], P('dp', 'grp')
Inputs may be any that keep to these rules, and one draw needn't show every extreme that they name: The tokens of one row have a common scale, and so have those of one feature. A device's live rows are the sum of its lengths; rows after them are padding. Within the devices sharing a dp index, live rows fill ceil(live rows / 32) blocks on each device and 32 blocks in all. dest is -1 exactly for a device's blocks past its live rows and an owner along grp otherwise. Within the devices sharing a dp index, every owner receives exactly 2 blocks and no device sends more than 1 block to one owner.
All inputs are finite; a program needn't handle non-finite values.
Results may differ from a plain program's by a relative error of at most 0.0049.
Values may be sent and summed in bfloat16 or wider, within the bound.
No kernel may reach another device: no remote copies, remote signals or barrier semaphores. Data moves between devices by JAX's collectives and lax.ppermute only.
A program may use at most 64 MiB of HBM per device.

v0:
```python
import jax
import jax.numpy as jnp
from jax import lax
from jax.sharding import PartitionSpec as P

BLK = 32
OWN_BLK = 2


EPS = 1e-06


def in_one_piece(arrays, axis, dim, along):
    widths = [a.shape[along] for a in arrays]
    both = jnp.concatenate(arrays, axis=along)
    result = lax.all_gather(both, axis, axis=dim, tiled=True)
    return tuple(jnp.split(result, [sum(widths[:k]) for k in range(1, len(widths))], axis=along))


def group_layout(dest_all, own_blocks):
    groups, slots_in = dest_all.shape
    flat_dest = dest_all.reshape(-1)
    flat_index = jnp.arange(groups * slots_in, dtype=jnp.int32)
    earlier = flat_index[None, :] < flat_index[:, None]
    same_dest = flat_dest[:, None] == flat_dest[None, :]
    source = flat_index // slots_in
    owner_rank = jnp.sum((same_dest & earlier).astype(jnp.int32), axis=1)
    pair_rank = jnp.sum(
        (same_dest & earlier & (source[:, None] == source[None, :])).astype(jnp.int32), axis=1
    )
    matches = (flat_dest[:, None, None] == jnp.arange(groups, dtype=jnp.int32)[None, :, None]) & (
        owner_rank[:, None, None] == jnp.arange(own_blocks, dtype=jnp.int32)[None, None, :]
    )
    picked = jnp.sum(jnp.where(matches, flat_index[:, None, None], 0), axis=0)
    return (picked, pair_rank)


def local_onehot(lens_row, count):
    doc_ends = jnp.cumsum(lens_row)
    position = jnp.arange(count, dtype=jnp.int32)
    doc_index = jnp.sum((position[:, None] >= doc_ends[None, :]).astype(jnp.int32), axis=1)
    is_live = position < doc_ends[-1]
    return (
        doc_index[:, None] == jnp.arange(lens_row.shape[0], dtype=jnp.int32)[None, :]
    ) & is_live[:, None]


def doc_squares(rows, onehot):
    widened = rows.astype(jnp.float32)
    square = jnp.sum(widened * widened, axis=1)
    return jnp.sum(jnp.where(onehot, square[:, None], 0.0), axis=0)


def apply_scale(rows, onehot, totals, lens_flat, gain):
    features = rows.shape[1]
    mean_square = totals / (jnp.maximum(lens_flat, 1).astype(jnp.float32) * features)
    inverse = lax.rsqrt(mean_square + EPS)
    scale = jnp.sum(jnp.where(onehot, inverse[None, :], 0.0), axis=1)
    return (rows.astype(jnp.float32) * scale[:, None] * gain[None, :]).astype(jnp.bfloat16)


def fold_rows(rows_all, weight):
    return jnp.dot(
        rows_all,
        lax.all_gather(weight, "dp", axis=0, tiled=True),
        preferred_element_type=jnp.float32,
    ).astype(jnp.bfloat16)


def per_device(tokens, lengths, dest, gain, weight):
    groups = lax.axis_size("grp")
    slots_in = 2 * OWN_BLK
    features = tokens.shape[1]
    pair_most = max(1, (slots_in + groups - 1) // groups)
    lens_all, dest_all = in_one_piece((lengths, dest), "grp", 0, 1)
    picked, pair_rank = group_layout(dest_all, OWN_BLK)
    my_index = lax.axis_index("grp")
    my_blocks = lax.dynamic_index_in_dim(picked, my_index, 0, keepdims=False)
    source_onehot = local_onehot(lengths[0], tokens.shape[0])
    source_totals = doc_squares(tokens, source_onehot)
    outgoing = apply_scale(tokens, source_onehot, source_totals, lengths[0], gain)
    my_dest = dest[0]
    local_index = jnp.arange(slots_in, dtype=jnp.int32)
    my_pair = jnp.sum(
        (
            (my_dest[:, None] == my_dest[None, :]) & (local_index[None, :] < local_index[:, None])
        ).astype(jnp.int32),
        axis=1,
    )
    slot_ids = jnp.arange(groups * pair_most, dtype=jnp.int32)
    send_pick = (my_dest[None, :] == (slot_ids // pair_most)[:, None]) & (
        my_pair[None, :] == (slot_ids % pair_most)[:, None]
    )
    parcel = jnp.dot(
        send_pick.astype(jnp.bfloat16),
        outgoing.reshape(slots_in, BLK * features),
        preferred_element_type=jnp.float32,
    ).astype(jnp.bfloat16)
    arrived = lax.all_to_all(parcel, "grp", split_axis=0, concat_axis=0, tiled=True)
    take_slot = my_blocks // slots_in * pair_most + pair_rank[my_blocks]
    take_onehot = (take_slot[:, None] == slot_ids[None, :]).astype(jnp.bfloat16)
    owned_rows = jnp.dot(take_onehot, arrived, preferred_element_type=jnp.float32).astype(
        jnp.bfloat16
    )
    owned_rows = owned_rows.reshape(OWN_BLK * BLK, features)
    rows_all = lax.all_gather(owned_rows, "grp", axis=0, tiled=True)
    return fold_rows(rows_all, weight)


def solution(mesh):
    placed = (
        P(("grp", "dp"), None),
        P(("grp", "dp"), None),
        P(("grp", "dp"), None),
        P(),
        P("dp", "grp"),
    )
    return jax.shard_map(
        per_device, mesh=mesh, in_specs=placed, out_specs=P("dp", "grp"), check_vma=False
    )
```

profile of v0, /device:TPU:1, one launch (start us, length us, event | category | flops | bytes accessed | tf_op | source)
XLA Modules:
  0.0 362.2 jit_solution(12504840859904070301)
XLA Ops:
  6.5 0.8 reduce-window.4
  7.4 0.6 slice.4
  8.0 0.6 iota_compare_fusion.7
  8.6 0.1 convert_reduce_fusion.2
  8.7 1.4 fusion.3
  10.1 0.1 select_reduce_fusion.2
  10.3 0.7 rsqrt_bitcast_fusion
  10.9 0.1 select_reduce_fusion.1
  11.0 1.5 fusion.5
  12.5 0.7 reshape.164
  13.2 0.2 convert_reduce_fusion.3
  13.4 2.9 fusion
  16.3 0.5 broadcast.230
  16.8 6.2 %reduce.3 = bf16[16,114688]{1,0:T(8,128)(2,1)} reduce(bf16[16,1,114688]{2,0,1:T(8,128)(2,1)} %fusion, bf16[]{:T(256)} %broadcast.230), dimensions={1}, to_apply=%copy.21.reduce_sub_computation | reduce | bytes 7340034 | tf_op jit(solution)/shard_map/all_to_all | solution.py:99
  23.0 5.9 %reshape.178 = bf16[16,2,57344]{2,1,0:T(2,128)(2,1)} reshape(bf16[16,114688]{1,0:T(8,128)(2,1)} %reduce.3) | data formatting | bytes 7340032
  28.9 15.9 %all-to-all-start = ((bf16[16,2,57344]{2,1,0:T(2,128)(2,1)}), bf16[16,2,57344]{2,1,0:T(2,128)(2,1)}, u32[]{:S(2)}, u32[]{:S(2)}) async-start(bf16[16,2,57344]{2,1,0:T(2,128)(2,1)} %reshape.178), calls=%async_computation | async-start | bytes 7340032 | tf_op jit(solution)/shard_map/all_to_all | solution.py:99
  44.9 0.0 all-gather.6.cloned.1.call-start
  44.9 0.7 all-gather.6.cloned.1.call-update
  45.7 0.1 add_bitcast_fusion
  45.7 176.0 %all-gather = s32[16,1,8]{2,1,0:T(1,128)S(1)} all-gather(s32[1,1,8]{2,1,0:T(1,128)S(1)} %add_bitcast_fusion), channel_id=1, replica_groups=mesh['grp'=16,'dp'=32] {'grp'}, dimensions={0}, use_global_device_ids=true | all-gather | bytes 544 | tf_op jit(solution)/shard_map/all_gather | solution.py:16
  221.7 0.1 copy.19
  221.8 0.1 copy.20
  221.9 0.1 eq.134
  222.0 0.2 convert_reduce_fusion.1
  222.2 0.1 select_reduce_fusion
  222.3 0.2 dynamic-slice_reduce_fusion
  222.5 0.6 gather_fusion
  223.2 12.0 %reshape.179 = bf16[16,1,114688]{2,1,0:T(2,128)(2,1)} reshape(bf16[16,2,57344]{2,1,0:T(2,128)(2,1)} %all-to-all-done) | data formatting | bytes 7340032
  235.2 7.2 %convolution_convert_fusion.1 = bf16[2,114688]{1,0:T(2,128)(2,1)S(1)} fusion(bf16[16,1,114688]{2,1,0:T(2,128)(2,1)} %reshape.179, s32[2]{0:T(128)S(1)} %fusion.17), kind=kOutput, calls=%fused_computation.3 | convolution fusion | flops 7569440 | bytes 4128776 | tf_op jit(solution)/shard_map/dot_general | solution.py:102
  242.4 1.2 reshape.165
  243.7 101.4 %all-gather.4.cloned.1.call-done = bf16[1024,3584]{1,0:T(8,128)(2,1)} async-done(((bf16[64,3584]{1,0:T(8,128)(2,1)}), bf16[1024,3584]{1,0:T(8,128)(2,1)}) %all-gather.4.cloned.1.call-update) | async-done | bytes 7340048 | tf_op jit(solution)/shard_map/all_gather | solution.py:106
  345.1 10.3 %convolution_convert_fusion.2 = bf16[1024,640]{1,0:T(8,128)(2,1)} fusion(bf16[1024,3584]{1,0:T(8,128)(2,1)} %all-gather.4.cloned.1.call-done, bf16[3584,640]{1,0:T(8,128)(2,1)} %all-gather.6.cloned.1.call-done), kind=kOutput, calls=%fused_computation.11 | convolution fusion | flops 4698275840 | bytes 13238272 | tf_op jit(solution)/shard_map/dot_general | solution.py:63
  (16 shorter events, 0.1 us)
Async XLA Ops:
  6.5 6.6 %copy-start = (s32[1,4]{1,0:T(1,128)S(1)}, s32[1,4]{1,0:T(1,128)}, u32[]{:S(2)}) copy-start(s32[1,4]{1,0:T(1,128)} %param.7) | copy-start | bytes 52
  28.9 16.7 %copy-start.1 = (s32[1,4]{1,0:T(1,128)S(1)}, s32[1,4]{1,0:T(1,128)}, u32[]{:S(2)}) copy-start(s32[1,4]{1,0:T(1,128)} %param.6) | copy-start | bytes 52
  28.9 194.3 %all-to-all-start = ((bf16[16,2,57344]{2,1,0:T(2,128)(2,1)}), bf16[16,2,57344]{2,1,0:T(2,128)(2,1)}, u32[]{:S(2)}, u32[]{:S(2)}) async-start(bf16[16,2,57344]{2,1,0:T(2,128)(2,1)} %reshape.178), calls=%async_computation | async-start | bytes 7340032 | tf_op jit(solution)/shard_map/all_to_all | solution.py:99
  44.9 198.8 %all-gather.6.cloned.1.call-start = ((), (), s32[]{:S(2)}) async-start(), calls=%async_computation.2 | async-start | bytes 4730880 | tf_op jit(solution)/shard_map/all_gather | solution.py:65
  45.6 299.5 %all-gather.4.cloned.1.call-start = ((), (), s32[]{:S(2)}) async-start(), calls=%async_computation.1 | async-start | bytes 7798784 | tf_op jit(solution)/shard_map/all_gather | solution.py:106
Sparse Core Ops, SparseCore 0:
  48.9 63.6 all-gather.5
  243.7 101.3 all-gather.3
where the time goes:
time: 363 us; the launch traced here: 362 us
  blocking collectives  176 us (48%)
  waiting for transfers between devices  102 us (28%)
  local copies, waits for them, and re-layouts  22 us (6%)
  matrix products  20.3 us (6%)
  starting transfers between devices  16 us (4%)
  between operations  13.5 us (4%)
  other arithmetic  12.2 us (3%)
    all_gather x1, blocking collectives, in_one_piece(): result = lax.all_gather(both, axis, axis=dim, tiled=True)  176 us
    all_gather x1, waiting for transfers between devices, per_device(): rows_all = lax.all_gather(owned_rows, 'grp', axis=0, tiled=True)  101 us
    unnamed x6, local copies, waits for them, and re-layouts  18 us
    all_to_all x1, starting transfers between devices, per_device(): lax.all_to_all(parcel, 'grp', split_axis=0, concat_axis=0, tiled=True)  15.9 us
    dot_general x1, matrix products, fold_rows(): jnp.dot(rows_all, lax.all_gather(weight, 'dp', axis=0, tiled=True), prefe...  10.3 us
  transfers between devices with their start and end apart: 3, of which 1 were waited for; matrix products, arithmetic and copies ran while one was open for 6% of the time, Pallas kernels for 0%

commit v1 on v0

v1 whole, which is shorter than its diff:
```python
import jax
import jax.numpy as jnp
from jax import lax
from jax.experimental import pallas as pl
from jax.experimental.pallas import tpu as pltpu
from jax.sharding import PartitionSpec as P

BLK = 32
OWN_BLK = 2
EPS = 1e-06
LANES = 128


def norm_kernel(lens_ref, dest_ref, tokens_ref, gain_ref, *outs):
    rows, features = tokens_ref.shape
    slots = rows // BLK
    unit = 2
    pieces = BLK // unit
    per_piece = slots * unit
    x = tokens_ref[...].astype(jnp.float32)
    square = jnp.sum(x * x, axis=1, keepdims=True)
    row = lax.broadcasted_iota(jnp.int32, (rows, 1), 0)
    scale = jnp.zeros((rows, 1), jnp.float32)
    start = jnp.int32(0)
    for c in range(lens_ref.shape[1]):
        size = lens_ref[0, c]
        inside = (row >= start) & (row < start + size)
        total = jnp.sum(jnp.where(inside, square, 0.0), axis=0, keepdims=True)
        count = jnp.full((1, 1), jnp.maximum(size, 1) * features, jnp.int32).astype(jnp.float32)
        inverse = lax.rsqrt(total / count + EPS)
        scale = scale + jnp.where(inside, inverse, 0.0)
        start = start + size
    normed = (x * scale * gain_ref[...]).astype(jnp.bfloat16)
    to = lax.broadcasted_iota(jnp.int32, (rows, rows), 0)
    frm = lax.broadcasted_iota(jnp.int32, (rows, rows), 1)
    want = (to % per_piece) // unit * BLK + (to // per_piece) * unit + to % unit
    perm = (want == frm).astype(jnp.float32).astype(jnp.bfloat16)
    mixed = jnp.dot(perm, normed, preferred_element_type=jnp.float32).astype(jnp.bfloat16)
    at = 0
    for n, out in enumerate(outs):
        width = out.shape[1] - (LANES if n == 0 else 0)
        out[:, :width] = mixed[:, at : at + width]
        at += width
    slot = (lax.broadcasted_iota(jnp.int32, (rows, LANES), 0) % per_piece) // unit
    owner = jnp.full((rows, LANES), dest_ref[0, 0], jnp.int32)
    for k in range(1, slots):
        owner = jnp.where(slot == k, dest_ref[0, k], owner)
    outs[0][:, outs[0].shape[1] - LANES :] = owner.astype(jnp.float32).astype(jnp.bfloat16)


def place_kernel(groups, data_ref, out_ref):
    rows = data_ref.shape[0]
    picked, width = out_ref.shape
    owner = data_ref[:, width:].astype(jnp.float32)
    lane = lax.broadcasted_iota(jnp.int32, (rows, LANES), 1)
    same = ((owner == lane.astype(jnp.float32)) & (lane < groups)).astype(jnp.float32)
    to = lax.broadcasted_iota(jnp.int32, (rows, rows), 0)
    frm = lax.broadcasted_iota(jnp.int32, (rows, rows), 1)
    before = ((frm // 2 < to // 2) & (frm % 2 == 0)).astype(jnp.float32).astype(jnp.bfloat16)
    earlier = jnp.dot(before, same.astype(jnp.bfloat16), preferred_element_type=jnp.float32)
    rank = jnp.sum(earlier * same, axis=1, keepdims=True)
    live = jnp.sum(same, axis=1, keepdims=True) > 0.5
    half = (lax.broadcasted_iota(jnp.int32, (rows, 1), 0) % 2).astype(jnp.float32)
    target = (owner[:, :1] * OWN_BLK + rank) * 2.0 + half
    spot = lax.broadcasted_iota(jnp.int32, (rows, picked), 1).astype(jnp.float32)
    pick = ((spot == target) & live).astype(jnp.float32).astype(jnp.bfloat16)
    out_ref[...] = lax.dot_general(
        pick, data_ref[:, :width], (((0,), (0,)), ((), ())), preferred_element_type=jnp.float32
    ).astype(jnp.bfloat16)


CHUNKS = 4


def project_kernel(x_hbm, w_ref, out_hbm, x_buf, y_buf, in_sem, out_sem):
    pieces, picked, depth = x_hbm.shape
    part = picked // CHUNKS
    height = pieces * part

    def load(q):
        return pltpu.make_async_copy(
            x_hbm.at[:, pl.ds(q * part, part), :], x_buf.at[q % 2], in_sem.at[q % 2]
        )

    def store(q):
        return pltpu.make_async_copy(
            y_buf.at[q % 2], out_hbm.at[pl.ds(q * height, height), :], out_sem.at[q % 2]
        )

    to = lax.broadcasted_iota(jnp.int32, (height, height), 0)
    frm = lax.broadcasted_iota(jnp.int32, (height, height), 1)
    want = (to % BLK) // 2 * part + (to // BLK) * 2 + to % 2
    perm = (want == frm).astype(jnp.float32).astype(jnp.bfloat16)
    load(0).start()
    for q in range(CHUNKS):
        if q + 1 < CHUNKS:
            load(q + 1).start()
        load(q).wait()
        x = x_buf[q % 2].reshape(height, depth)
        y = jnp.dot(x, w_ref[...], preferred_element_type=jnp.float32).astype(jnp.bfloat16)
        if q >= 2:
            store(q - 2).wait()
        y_buf[q % 2] = jnp.dot(perm, y, preferred_element_type=jnp.float32).astype(jnp.bfloat16)
        store(q).start()
    for q in range(CHUNKS - 2, CHUNKS):
        store(q).wait()


def cost(flops, nbytes):
    return pl.CostEstimate(flops=flops, bytes_accessed=nbytes, transcendentals=0)


VM = pl.BlockSpec(memory_space=pltpu.VMEM)
SM = pl.BlockSpec(memory_space=pltpu.SMEM)
HB = pl.BlockSpec(memory_space=pltpu.HBM)
MIB = 1024 * 1024


def per_device(tokens, lengths, dest, gain, weight):
    groups = lax.axis_size("grp")
    rows, features = tokens.shape
    cols = weight.shape[1]
    own = groups * OWN_BLK * 2
    (mixed,) = pl.pallas_call(
        norm_kernel,
        out_shape=[jax.ShapeDtypeStruct((rows, features + LANES), jnp.bfloat16)],
        in_specs=[SM, SM, VM, VM],
        out_specs=[VM],
        compiler_params=pltpu.CompilerParams(vmem_limit_bytes=16 * MIB),
        cost_estimate=cost(2 * rows * rows * features, 4 * rows * features),
        name="norm",
    )(lengths, dest, tokens, gain.reshape(1, features))
    with jax.named_scope("swap"):
        sent = lax.all_to_all(mixed, "grp", split_axis=0, concat_axis=0, tiled=True)
    owned = pl.pallas_call(
        lambda *refs: place_kernel(groups, *refs),
        out_shape=jax.ShapeDtypeStruct((own, features), jnp.bfloat16),
        in_specs=[VM],
        out_specs=VM,
        compiler_params=pltpu.CompilerParams(vmem_limit_bytes=16 * MIB),
        cost_estimate=cost(2 * rows * own * features, 3 * rows * features),
        name="place",
    )(sent)
    with jax.named_scope("wide"):
        w_all = lax.all_gather(weight, "dp", axis=0, tiled=True)
    owned, w_all = lax.optimization_barrier((owned, w_all))
    with jax.named_scope("spread"):
        x_all = lax.all_gather(owned, "grp", axis=0, tiled=True)
    height = groups * own // CHUNKS
    return pl.pallas_call(
        project_kernel,
        out_shape=jax.ShapeDtypeStruct((groups * own, cols), jnp.bfloat16),
        in_specs=[HB, VM],
        out_specs=HB,
        scratch_shapes=[
            pltpu.VMEM((2, groups, own // CHUNKS, features), jnp.bfloat16),
            pltpu.VMEM((2, height, cols), jnp.bfloat16),
            pltpu.SemaphoreType.DMA((2,)),
            pltpu.SemaphoreType.DMA((2,)),
        ],
        compiler_params=pltpu.CompilerParams(vmem_limit_bytes=56 * MIB),
        cost_estimate=cost(2 * groups * own * features * cols, 2 * groups * own * features),
        name="project",
    )(x_all.reshape(groups, own, features), w_all)


def solution(mesh):
    placed = (
        P(("grp", "dp"), None),
        P(("grp", "dp"), None),
        P(("grp", "dp"), None),
        P(),
        P("dp", "grp"),
    )
    return jax.shard_map(
        per_device, mesh=mesh, in_specs=placed, out_specs=P("dp", "grp"), check_vma=False
    )
```

time: 363 us -> 193 us (0.53)
  blocking collectives: 176 us -> 58.1 us
  matrix products: 20.3 us -> 0 us
  local copies, waits for them, and re-layouts: 22 us -> 3.21 us
  starting transfers between devices: 16 us -> 0.04 us
  Pallas kernels: 0 us -> 14.6 us
  other arithmetic: 12.2 us -> 0 us
    all_gather x1 -> x0, blocking collectives: 176 us -> none  [in_one_piece(): result = lax.all_gather(both, axis, axis=dim, tiled=True)]
    all_to_all x0 -> x1, blocking collectives: none -> 58.1 us  [per_device(): sent = lax.all_to_all(mixed, 'grp', split_axis=0, concat_axis=0, tiled=True)]
    dot_general x3 -> x0, matrix products: 20.3 us -> none  [the longest x1 10.3 us: fold_rows(): jnp.dot(rows_all, lax.all_gather(weight, 'dp', axis=0, tiled=True), prefe...]
    all_to_all x1 -> x0, starting transfers between devices: 15.9 us -> none  [per_device(): lax.all_to_all(parcel, 'grp', split_axis=0, concat_axis=0, tiled=True)]
    unnamed x6, local copies, waits for them, and re-layouts: 18 us -> 2.48 us
    pallas_call x0 -> x3, Pallas kernels: none -> 14.6 us  [the longest x1 11.9 us: per_device(): pl.pallas_call(project_kernel, out_shape=jax.ShapeDtypeStruct((groups * o...]
    all_to_all x1 -> x0, other arithmetic: 6.21 us -> none  [per_device(): lax.all_to_all(parcel, 'grp', split_axis=0, concat_axis=0, tiled=True)]
  transfers between devices with their start and end apart: 3 -> 2, of which waited for: 1 -> 2; matrix products, arithmetic and copies ran while one was open for 6% -> 0% of each run, Pallas kernels for 0% -> 1%
where the time goes in v1:
time: 193 us
  waiting for transfers between devices  104 us (54%)
  blocking collectives  58.1 us (30%)
  Pallas kernels  14.6 us (8%)
  between operations  13.4 us (7%)
  local copies, waits for them, and re-layouts  3.21 us (2%)
    all_gather x1, waiting for transfers between devices, per_device(): x_all = lax.all_gather(owned, 'grp', axis=0, tiled=True)  96.4 us
    all_to_all x1, blocking collectives, per_device(): sent = lax.all_to_all(mixed, 'grp', split_axis=0, concat_axis=0, tiled=True)  58.1 us
    pallas_call x1, Pallas kernels, per_device(): pl.pallas_call(project_kernel, out_shape=jax.ShapeDtypeStruct((groups * o...  11.9 us
    all_gather x1, waiting for transfers between devices, per_device(): w_all = lax.all_gather(weight, 'dp', axis=0, tiled=True)  6.65 us
  transfers between devices with their start and end apart: 2, of which 2 were waited for; matrix products, arithmetic and copies ran while one was open for 0% of the time, Pallas kernels for 1%

profile of v1, /device:TPU:1, one launch (start us, length us, event | category | flops | bytes accessed | tf_op | source)
XLA Modules:
  0.0 193.1 jit_solution(13341659233617846198)
XLA Ops:
  6.5 0.0 all-gather.3.cloned.1.call-start
  6.5 0.7 all-gather.3.cloned.1.call-update
  7.3 0.0 all-gather.5.cloned.1.call-start
  7.3 0.7 reshape.8.gain_ref
  8.0 0.0 copy-start
  8.0 1.2 copy-done
  9.2 0.0 copy-start.1
  9.2 0.7 copy-done.1
  9.9 0.0 copy-start.2
  9.9 0.7 copy-done.2
  10.5 1.3 norm.1
  11.8 58.1 %all_to_all.11 = bf16[16,8,3712]{2,1,0:T(8,128)(2,1)S(1)} all-to-all(bf16[16,8,3712]{2,1,0:T(8,128)(2,1)S(1)} %bitcast.3), channel_id=1, replica_groups=mesh['grp'=16,'dp'=32] {'grp'}, dimensions={0} | all-to-all | bytes 1900544 | tf_op jit(solution)/shard_map/swap/all_to_all | solution.py:134
  69.9 1.4 place.1
  71.3 6.7 %all-gather.3.cloned.1.call-done.w_ref = bf16[3584,640]{1,0:T(8,128)(2,1)} async-done(((bf16[112,640]{1,0:T(8,128)(2,1)}), bf16[3584,640]{1,0:T(8,128)(2,1)}) %all-gather.3.cloned.1.call-update) | async-done | bytes 4587536 | tf_op jit(solution)/shard_map/wide/all_gather | solution.py:145
  78.0 0.0 all-gather.5.cloned.1.call-update
  78.0 96.4 %all-gather.5.cloned.1.call-done = bf16[1024,3584]{1,0:T(8,128)(2,1)} async-done(((bf16[64,3584]{1,0:T(8,128)(2,1)}), bf16[1024,3584]{1,0:T(8,128)(2,1)}) %all-gather.5.cloned.1.call-update) | async-done | bytes 7340048 | tf_op jit(solution)/shard_map/spread/all_gather | solution.py:148
  174.4 11.9 %project.1 = bf16[1024,640]{1,0:T(8,128)(2,1)} custom-call(bf16[16,64,3584]{2,1,0:T(8,128)(2,1)} %bitcast.5, bf16[3584,640]{1,0:T(8,128)(2,1)} %all-gather.3.cloned.1.call-done.w_ref), custom_call_target="tpu_custom_call" | custom-call | flops 4697620480 | bytes 7340032 | tf_op jit(solution)/shard_map/project/pallas_call | solution.py:150
Async XLA Ops:
  6.5 71.4 %all-gather.3.cloned.1.call-start = ((), (), s32[]{:S(2)}) async-start(), calls=%async_computation.1 | async-start | bytes 4730880 | tf_op jit(solution)/shard_map/wide/all_gather | solution.py:145
  7.3 167.1 %all-gather.5.cloned.1.call-start = ((), (), s32[]{:S(2)}) async-start(), calls=%async_computation.2 | async-start | bytes 7798784 | tf_op jit(solution)/shard_map/spread/all_gather | solution.py:148
  8.0 1.2 copy-start
  9.2 0.7 copy-start.1
  9.9 0.7 copy-start.2
Sparse Core Ops, SparseCore 0:
  10.5 67.3 all-gather.2
  80.0 94.2 all-gather.4

commit v2 on v1

v2 whole, which is shorter than its diff:
```python
import jax
import jax.numpy as jnp
from jax import lax
from jax.experimental import pallas as pl
from jax.experimental.pallas import tpu as pltpu
from jax.sharding import PartitionSpec as P

BLK = 32
OWN_BLK = 2
EPS = 1e-06
LANES = 128


def norm_kernel(
    lens_hbm, dest_hbm, tokens_hbm, gain_hbm, out_ref, lens_ref, dest_ref, tokens_ref, gain_ref, sems
):
    copies = [
        pltpu.make_async_copy(src, dst, sems.at[n])
        for n, (src, dst) in enumerate(
            (
                (tokens_hbm, tokens_ref),
                (gain_hbm, gain_ref.at[0]),
                (lens_hbm, lens_ref),
                (dest_hbm, dest_ref),
            )
        )
    ]
    for copy in copies:
        copy.start()
    rows, features = tokens_ref.shape
    slots = rows // BLK
    unit = 2
    per_piece = slots * unit
    to = lax.broadcasted_iota(jnp.int32, (rows, rows), 0)
    frm = lax.broadcasted_iota(jnp.int32, (rows, rows), 1)
    want = (to % per_piece) // unit * BLK + (to // per_piece) * unit + to % unit
    perm = (want == frm).astype(jnp.float32).astype(jnp.bfloat16)
    for copy in copies:
        copy.wait()
    x = tokens_ref[...].astype(jnp.float32)
    square = jnp.sum(x * x, axis=1, keepdims=True)
    row = lax.broadcasted_iota(jnp.int32, (rows, 1), 0)
    scale = jnp.zeros((rows, 1), jnp.float32)
    start = jnp.int32(0)
    for c in range(lens_ref.shape[1]):
        size = lens_ref[0, c]
        inside = (row >= start) & (row < start + size)
        total = jnp.sum(jnp.where(inside, square, 0.0), axis=0, keepdims=True)
        count = jnp.full((1, 1), jnp.maximum(size, 1) * features, jnp.int32).astype(jnp.float32)
        inverse = lax.rsqrt(total / count + EPS)
        scale = scale + jnp.where(inside, inverse, 0.0)
        start = start + size
    normed = (x * scale * gain_ref[...]).astype(jnp.bfloat16)
    out_ref[:, :features] = jnp.dot(
        perm, normed, preferred_element_type=jnp.float32
    ).astype(jnp.bfloat16)
    slot = (lax.broadcasted_iota(jnp.int32, (rows, LANES), 0) % per_piece) // unit
    owner = jnp.full((rows, LANES), dest_ref[0, 0], jnp.int32)
    for k in range(1, slots):
        owner = jnp.where(slot == k, dest_ref[0, k], owner)
    out_ref[:, features:] = owner.astype(jnp.float32).astype(jnp.bfloat16)


def place_kernel(groups, data_ref, out_ref):
    rows = data_ref.shape[0]
    picked, width = out_ref.shape
    owner = data_ref[:, width:].astype(jnp.float32)
    lane = lax.broadcasted_iota(jnp.int32, (rows, LANES), 1)
    same = ((owner == lane.astype(jnp.float32)) & (lane < groups)).astype(jnp.float32)
    to = lax.broadcasted_iota(jnp.int32, (rows, rows), 0)
    frm = lax.broadcasted_iota(jnp.int32, (rows, rows), 1)
    before = ((frm // 2 < to // 2) & (frm % 2 == 0)).astype(jnp.float32).astype(jnp.bfloat16)
    earlier = jnp.dot(before, same.astype(jnp.bfloat16), preferred_element_type=jnp.float32)
    rank = jnp.sum(earlier * same, axis=1, keepdims=True)
    live = jnp.sum(same, axis=1, keepdims=True) > 0.5
    half = (lax.broadcasted_iota(jnp.int32, (rows, 1), 0) % 2).astype(jnp.float32)
    target = (owner[:, :1] * OWN_BLK + rank) * 2.0 + half
    spot = lax.broadcasted_iota(jnp.int32, (rows, picked), 1).astype(jnp.float32)
    pick = ((spot == target) & live).astype(jnp.float32).astype(jnp.bfloat16)
    out_ref[...] = lax.dot_general(
        pick, data_ref[:, :width], (((0,), (0,)), ((), ())), preferred_element_type=jnp.float32
    ).astype(jnp.bfloat16)


HALVES = 2
PARTS = 2
STEP = 512


TILE = 256


def join_kernel(side_ref, mine_ref, theirs_ref, out_ref, whole, sems):
    side = side_ref[0]
    first = pltpu.make_async_copy(mine_ref, whole.at[:, side], sems.at[0])
    second = pltpu.make_async_copy(theirs_ref, whole.at[:, 1 - side], sems.at[1])
    first.start()
    second.start()
    first.wait()
    second.wait()
    cols, depth = out_ref.shape
    flat = whole.reshape(depth, cols)
    for k in range(0, depth, TILE):
        out_ref[:, k : k + TILE] = flat[k : k + TILE, :].T


def project_kernel(x_hbm, w_hbm, out_hbm, x_buf, w_buf, y_buf, x_sem, w_sem, out_sem):
    depth = x_hbm.shape[2]
    halves, parts, pieces, picked, _ = x_buf.shape
    height = pieces * picked

    def load(q, s, n):
        if q == 0:
            cut = pl.ds(n * STEP, STEP)
        else:
            cut = pl.ds(0, depth)
        rows = pl.ds((q * parts + s) * picked, picked)
        return pltpu.make_async_copy(
            x_hbm.at[:, rows, cut], x_buf.at[q, s, :, :, cut], x_sem.at[q, s, n]
        )

    def weights(n):
        cut = pl.ds(n * STEP, STEP)
        return pltpu.make_async_copy(w_hbm.at[:, cut], w_buf.at[:, cut], w_sem.at[n])

    steps = depth // STEP
    for n in range(steps):
        weights(n).start()
        for s in range(parts):
            load(0, s, n).start()
    for q in range(1, halves):
        for s in range(parts):
            load(q, s, 0).start()
    to = lax.broadcasted_iota(jnp.int32, (height, height), 0)
    frm = lax.broadcasted_iota(jnp.int32, (height, height), 1)
    want = (to % BLK) // 2 * picked + (to // BLK) * 2 + to % 2
    perm = (want == frm).astype(jnp.float32).astype(jnp.bfloat16)
    across = (((1,), (1,)), ((), ()))
    stores = []
    for q in range(halves):
        total = None
        width = STEP if q == 0 else depth
        for n in range(depth // width):
            if q == 0:
                weights(n).wait()
            for s in range(parts):
                load(q, s, n).wait()
            low, high = n * width, (n + 1) * width
            x = x_buf[q, :, :, :, low:high].reshape(parts * height, width)
            term = lax.dot_general(
                w_buf[:, low:high], x, across, preferred_element_type=jnp.float32
            )
            total = term if total is None else total + term
        y = total.astype(jnp.bfloat16)
        for s in range(parts):
            k = q * parts + s
            y_buf[k] = lax.dot_general(
                perm,
                y[:, s * height : (s + 1) * height],
                across,
                preferred_element_type=jnp.float32,
            ).astype(jnp.bfloat16)
            store = pltpu.make_async_copy(
                y_buf.at[k], out_hbm.at[pl.ds(k * height, height), :], out_sem.at[k]
            )
            store.start()
            stores.append(store)
    for store in stores:
        store.wait()


def cost(flops, nbytes):
    return pl.CostEstimate(flops=flops, bytes_accessed=nbytes, transcendentals=0)


VM = pl.BlockSpec(memory_space=pltpu.VMEM)
SM = pl.BlockSpec(memory_space=pltpu.SMEM)
HB = pl.BlockSpec(memory_space=pltpu.HBM)
MIB = 1024 * 1024


def per_device(tokens, lengths, dest, gain, weight):
    groups = lax.axis_size("grp")
    rows, features = tokens.shape
    cols = weight.shape[1]
    own = groups * OWN_BLK * 2
    mixed = pl.pallas_call(
        norm_kernel,
        out_shape=jax.ShapeDtypeStruct((rows, features + LANES), jnp.bfloat16),
        in_specs=[HB, HB, HB, HB],
        out_specs=VM,
        scratch_shapes=[
            pltpu.SMEM(lengths.shape, jnp.int32),
            pltpu.SMEM(dest.shape, jnp.int32),
            pltpu.VMEM(tokens.shape, jnp.bfloat16),
            pltpu.VMEM((1, features), jnp.float32),
            pltpu.SemaphoreType.DMA((4,)),
        ],
        compiler_params=pltpu.CompilerParams(vmem_limit_bytes=65800000),
        cost_estimate=cost(2 * rows * rows * features, 4 * rows * features),
        name="norm",
    )(lengths, dest, tokens, gain)
    with jax.named_scope("swap"):
        sent = lax.all_to_all(mixed, "grp", split_axis=0, concat_axis=0, tiled=True)
    owned = pl.pallas_call(
        lambda *refs: place_kernel(groups, *refs),
        out_shape=jax.ShapeDtypeStruct((own, features), jnp.bfloat16),
        in_specs=[VM],
        out_specs=VM,
        compiler_params=pltpu.CompilerParams(vmem_limit_bytes=16 * MIB),
        cost_estimate=cost(2 * rows * own * features, 3 * rows * features),
        name="place",
    )(sent)
    owned, weight = lax.optimization_barrier((owned, weight))
    with jax.named_scope("spread"):
        x_all = lax.all_gather(owned, "grp", axis=0, tiled=True)
    with jax.named_scope("wide"):
        depth = weight.shape[0]
        cores = lax.axis_size("dp") // 2
        copies = jnp.broadcast_to(weight[None], (cores, depth, cols)).reshape(cores * depth, cols)
        same = [[2 * i + c for i in range(cores)] for c in range(2)]
        mine = lax.all_to_all(
            copies, "dp", split_axis=0, concat_axis=0, tiled=True, axis_index_groups=same
        )
        theirs = lax.ppermute(mine, "dp", [(d, d ^ 1) for d in range(2 * cores)])
        w_all = pl.pallas_call(
            join_kernel,
            out_shape=jax.ShapeDtypeStruct((cols, features), jnp.bfloat16),
            in_specs=[SM, HB, HB],
            out_specs=VM,
            scratch_shapes=[
                pltpu.VMEM((cores, 2, depth, cols), jnp.bfloat16),
                pltpu.SemaphoreType.DMA((2,)),
            ],
            compiler_params=pltpu.CompilerParams(vmem_limit_bytes=24 * MIB),
            cost_estimate=cost(0, 4 * cores * depth * cols * 2),
            name="join",
        )(
            lax.rem(lax.axis_index("dp"), 2).reshape(1),
            mine.reshape(cores, depth, cols),
            theirs.reshape(cores, depth, cols),
        )
    count = HALVES * PARTS
    picked = own // count
    return pl.pallas_call(
        project_kernel,
        out_shape=jax.ShapeDtypeStruct((groups * own, cols), jnp.bfloat16),
        in_specs=[HB, HB],
        out_specs=HB,
        scratch_shapes=[
            pltpu.VMEM((HALVES, PARTS, groups, picked, features), jnp.bfloat16),
            pltpu.VMEM((cols, features), jnp.bfloat16),
            pltpu.VMEM((count, groups * picked, cols), jnp.bfloat16),
            pltpu.SemaphoreType.DMA((HALVES, PARTS, features // STEP)),
            pltpu.SemaphoreType.DMA((features // STEP,)),
            pltpu.SemaphoreType.DMA((count,)),
        ],
        compiler_params=pltpu.CompilerParams(vmem_limit_bytes=56 * MIB),
        cost_estimate=cost(2 * groups * own * features * cols, 2 * groups * own * features),
        name="project",
    )(x_all.reshape(groups, own, features), w_all)


def solution(mesh):
    placed = (
        P(("grp", "dp"), None),
        P(("grp", "dp"), None),
        P(("grp", "dp"), None),
        P(),
        P("dp", "grp"),
    )
    return jax.shard_map(
        per_device, mesh=mesh, in_specs=placed, out_specs=P("dp", "grp"), check_vma=False
    )
```

time: 193 us -> 181 us (0.938)
  waiting for transfers between devices: 104 us -> 50.8 us
  blocking collectives: 58.1 us -> 88.7 us
  starting transfers between devices: 0.04 us -> 9.48 us
    all_gather x1, waiting for transfers between devices: 96.4 us -> 46.7 us  [per_device(): x_all = lax.all_gather(owned, 'grp', axis=0, tiled=True)]
    all_to_all x0 -> x1, blocking collectives: none -> 30.3 us  [per_device(): lax.all_to_all(copies, 'dp', split_axis=0, concat_axis=0, tiled=True, axi...]
    ppermute x0 -> x1, starting transfers between devices: none -> 9.48 us  [per_device(): theirs = lax.ppermute(mine, 'dp', [(d, d ^ 1) for d in range(2 * cores)])]
    all_gather x1 -> x0, waiting for transfers between devices: 6.65 us -> none  [per_device(): w_all = lax.all_gather(weight, 'dp', axis=0, tiled=True)]
    pallas_call x1 -> x2, Pallas kernels: 1.28 us -> 5.96 us  [the longest x1 3.07 us: per_device(): pl.pallas_call(join_kernel, out_shape=jax.ShapeDtypeStruct((cols, feature...]
    ppermute x0 -> x1, waiting for transfers between devices: none -> 4.17 us  [per_device(): theirs = lax.ppermute(mine, 'dp', [(d, d ^ 1) for d in range(2 * cores)])]
    pallas_call x1, Pallas kernels: 11.9 us -> 8.8 us  [per_device(): pl.pallas_call(project_kernel, out_shape=jax.ShapeDtypeStruct((groups * o...]
  transfers between devices with their start and end apart: 2 -> 2, of which waited for: 2 -> 2; matrix products, arithmetic and copies ran while one was open for 0% -> 0% of each run, Pallas kernels for 1% -> 2%
where the time goes in v2:
time: 181 us
  blocking collectives  88.7 us (49%)
  waiting for transfers between devices  50.8 us (28%)
  Pallas kernels  16.2 us (9%)
  between operations  13.5 us (7%)
  starting transfers between devices  9.48 us (5%)
  local copies, waits for them, and re-layouts  2.33 us (1%)
    all_to_all x1, blocking collectives, per_device(): sent = lax.all_to_all(mixed, 'grp', split_axis=0, concat_axis=0, tiled=True)  58.4 us
    all_gather x1, waiting for transfers between devices, per_device(): x_all = lax.all_gather(owned, 'grp', axis=0, tiled=True)  46.7 us
    all_to_all x1, blocking collectives, per_device(): lax.all_to_all(copies, 'dp', split_axis=0, concat_axis=0, tiled=True, axi...  30.3 us
    ppermute x1, starting transfers between devices, per_device(): theirs = lax.ppermute(mine, 'dp', [(d, d ^ 1) for d in range(2 * cores)])  9.48 us
    pallas_call x1, Pallas kernels, per_device(): pl.pallas_call(project_kernel, out_shape=jax.ShapeDtypeStruct((groups * o...  8.8 us
    ppermute x1, waiting for transfers between devices, per_device(): theirs = lax.ppermute(mine, 'dp', [(d, d ^ 1) for d in range(2 * cores)])  4.17 us
  transfers between devices with their start and end apart: 2, of which 2 were waited for; matrix products, arithmetic and copies ran while one was open for 0% of the time, Pallas kernels for 2%

profile of v2, /device:TPU:1, one launch (start us, length us, event | category | flops | bytes accessed | tf_op | source)
XLA Modules:
  0.0 181.0 jit_solution(100438277420714342)
XLA Ops:
  6.5 0.0 all-gather.2.cloned.1.call-start
  6.5 2.9 %norm.1 = bf16[128,3712]{1,0:T(8,128)(2,1)} custom-call(s32[1,4]{1,0:T(1,128)} %lens_hbm.1, s32[1,4]{1,0:T(1,128)} %dest_hbm.1, bf16[128,3584]{1,0:T(8,128)(2,1)} %tokens_hbm.1, f32[3584]{0:T(1024)} %gain_hbm.1), custom_call_target="tpu_custom_call" | custom-call | flops 117440512 | bytes 1835008 | tf_op jit(solution)/shard_map/norm/pallas_call | solution.py:187
  9.4 0.0 copy-start.1
  9.4 58.4 %all_to_all.20 = bf16[16,8,3712]{2,1,0:T(8,128)(2,1)S(1)} all-to-all(bf16[16,8,3712]{2,1,0:T(8,128)(2,1)} %bitcast.8), channel_id=1, replica_groups=mesh['grp'=16,'dp'=32] {'grp'}, dimensions={0} | all-to-all | bytes 1900544 | tf_op jit(solution)/shard_map/swap/all_to_all | solution.py:204
  67.9 1.4 place.1
  69.3 0.0 all-gather.2.cloned.1.call-update
  69.3 0.0 copy-done.1
  69.3 0.2 broadcast_in_dim.2
  69.5 30.3 %all_to_all.21.mine_ref = bf16[16,112,640]{2,1,0:T(8,128)(2,1)S(1)} all-to-all(bf16[16,112,640]{2,1,0:T(8,128)(2,1)S(1)} %broadcast_in_dim.2), channel_id=1, replica_groups={{0,2,4,6,8,10,12,14,16,18,20,22,24,26,28,30},{1,3,5,7,9,11,13,15,17,19,..., dimensions={0} | all-to-all | bytes 4587520 | tf_op jit(solution)/shard_map/wide/all_to_all | solution.py:222
  99.8 9.5 %collective-permute-start = (bf16[1792,640]{1,0:T(8,128)(2,1)S(1)}, bf16[1792,640]{1,0:T(8,128)(2,1)}, u32[]{:S(2)}, u32[]{:S(2)}) collective-permute-start(bf16[1792,640]{1,0:T(8,128)(2,1)S(1)} %bitcast.6), channel_id=1, source_target_pairs={{0,1},{1,0},{2,3},{3,2},{4,5},{5,4},{6,7},{7,6},{8,9},{9,8},{10,11... | collective-permute-start | bytes 6881288 | tf_op jit(solution)/shard_map/wide/ppermute | solution.py:225
  109.3 4.2 %collective-permute-done = bf16[1792,640]{1,0:T(8,128)(2,1)} collective-permute-done((bf16[1792,640]{1,0:T(8,128)(2,1)S(1)}, bf16[1792,640]{1,0:T(8,128)(2,1)}, u32[]{:S(2)}, u32[]{:S(2)}) %collective-permute-start) | collective-permute-done | bytes 2293792 | tf_op jit(solution)/shard_map/wide/ppermute | solution.py:225
  113.4 3.1 %join.1.w_hbm = bf16[640,3584]{1,0:T(8,128)(2,1)S(1)} custom-call(s32[1]{0:T(128)} %bitcast.3.side_ref, bf16[16,112,640]{2,1,0:T(8,128)(2,1)S(1)} %all_to_all.21.mine_ref, bf16[16,112,640]{2,1,0:T(8,128)(2,1)} %bitcast.5.theirs_ref), custom_call_target="tpu_custom_call" | custom-call | bytes 9175040 | tf_op jit(solution)/shard_map/wide/join/pallas_call | solution.py:226
  116.5 0.0 copy-start
  116.5 2.1 %copy-done = bf16[640,3584]{1,0:T(8,128)(2,1)} copy-done((bf16[640,3584]{1,0:T(8,128)(2,1)}, bf16[640,3584]{1,0:T(8,128)(2,1)S(1)}, u32[]{:S(2)}) %copy-start) | copy-done | bytes 4587544
  118.7 46.7 %all-gather.2.cloned.1.call-done = bf16[1024,3584]{1,0:T(8,128)(2,1)} async-done(((bf16[64,3584]{1,0:T(8,128)(2,1)}), bf16[1024,3584]{1,0:T(8,128)(2,1)}) %all-gather.2.cloned.1.call-update) | async-done | bytes 7340048 | tf_op jit(solution)/shard_map/spread/all_gather | solution.py:216
  165.3 8.8 %project.1 = bf16[1024,640]{1,0:T(8,128)(2,1)} custom-call(bf16[16,64,3584]{2,1,0:T(8,128)(2,1)} %bitcast.9, bf16[640,3584]{1,0:T(8,128)(2,1)} %copy-done), custom_call_target="tpu_custom_call" | custom-call | flops 4697620480 | bytes 7340032 | tf_op jit(solution)/shard_map/project/pallas_call | solution.py:245
Async XLA Ops:
  6.5 158.8 %all-gather.2.cloned.1.call-start = ((), (), s32[]{:S(2)}) async-start(), calls=%async_computation.2 | async-start | bytes 7798784 | tf_op jit(solution)/shard_map/spread/all_gather | solution.py:216
  9.4 59.9 %copy-start.1 = (bf16[112,640]{1,0:T(8,128)(2,1)S(1)}, bf16[112,640]{1,0:T(8,128)(2,1)}, u32[]{:S(2)}) copy-start(bf16[112,640]{1,0:T(8,128)(2,1)} %param.9) | copy-start | bytes 430084
  99.8 13.7 %collective-permute-start = (bf16[1792,640]{1,0:T(8,128)(2,1)S(1)}, bf16[1792,640]{1,0:T(8,128)(2,1)}, u32[]{:S(2)}, u32[]{:S(2)}) collective-permute-start(bf16[1792,640]{1,0:T(8,128)(2,1)S(1)} %bitcast.6), channel_id=1, source_target_pairs={{0,1},{1,0},{2,3},{3,2},{4,5},{5,4},{6,7},{7,6},{8,9},{9,8},{10,11... | collective-permute-start | bytes 6881288 | tf_op jit(solution)/shard_map/wide/ppermute | solution.py:225
  116.5 2.1 %copy-start = (bf16[640,3584]{1,0:T(8,128)(2,1)}, bf16[640,3584]{1,0:T(8,128)(2,1)S(1)}, u32[]{:S(2)}) copy-start(bf16[640,3584]{1,0:T(8,128)(2,1)S(1)} %join.1.w_hbm) | copy-start | bytes 13762564
Sparse Core Ops, SparseCore 0:
  69.4 95.8 all-gather.1
